TPU v7x, 32 devices: a whole 2x2x4 slice. The times are simulated.
32 devices in a mesh: grid: 8 (over y, x, core), band: 4 (over z).
Axes of the slice: x: 2, y: 2, z: 4, core: 2. Of those that a mesh axis runs over, the one named last changes fastest.
Arguments:
- orbitals: bfloat16 [32, 64, 64, 128], P('band', 'grid'), may hold values from -6 to 6
- occupation: int32 [32], P('band'), may hold values from 1 to 2
- spin_of_band: int32 [32], P('band'), may hold values from 0 to 1
- ionic_charge: float32 [64, 64, 128], P('grid'), may hold values from 0.3 to 3
Outputs:
- potential: float32 [2, 64, 64, 128], P(None, 'grid')
- applied: bfloat16 [32, 64, 64, 128], P('band', 'grid')
All inputs are finite; a program needn't handle non-finite values.
Results may differ from a plain program's by a relative error of at most 0.001.
Values sent between devices are 32-bit elements; how exact they have to be, the bound alone decides.
A program may use at most 64 MiB of HBM per device.

v0:
```python
import math
import jax
import jax.numpy as jnp
from jax import lax
from jax.sharding import PartitionSpec as P

NZ = 64
spacing = 0.25
highest = lax.Precision.HIGHEST


def tables(count):
    index = jnp.arange(count, dtype=jnp.int32)
    product = index[:, None] * index[None, :] % count
    angle = 2.0 * math.pi * product.astype(jnp.float32) / count
    return (jnp.cos(angle), jnp.sin(angle))


def signed_sq(index, count):
    signed = jnp.where(index < count // 2, index, index - count).astype(jnp.float32)
    wave = 2.0 * math.pi * signed / (count * spacing)
    return wave * wave


def kernel_at(depth, row_index, rows, col_index, cols):
    g_sq = signed_sq(jnp.arange(depth, dtype=jnp.int32), depth)[:, None, None]
    g_sq = g_sq + signed_sq(row_index, rows)[None, :, None]
    g_sq = g_sq + signed_sq(col_index, cols)[None, None, :]
    return jnp.where(g_sq > 0, 4.0 * math.pi / jnp.where(g_sq > 0, g_sq, 1.0), 0.0)


def along(table, field, form):
    return jnp.einsum(form, table, field, precision=highest)


def forward_y(cos_y, sin_y, real_x, imag_x):
    form_y = "ky,zyx->zkx"
    real_y = along(cos_y, real_x, form_y) + along(sin_y, imag_x, form_y)
    imag_y = along(cos_y, imag_x, form_y) - along(sin_y, real_x, form_y)
    return (real_y, imag_y)


def inverse_y(cos_y, sin_y, real_k, imag_k):
    form_y = "ky,zyx->zkx"
    plane_real = along(cos_y, real_k, form_y) - along(sin_y, imag_k, form_y)
    plane_imag = along(cos_y, imag_k, form_y) + along(sin_y, real_k, form_y)
    return (plane_real, plane_imag)


def z_kernel(cos_z, sin_z, moved, kernel):
    form_z = "kz,zyx->kyx"
    real_z = along(cos_z, moved[0], form_z) + along(sin_z, moved[1], form_z)
    imag_z = along(cos_z, moved[1], form_z) - along(sin_z, moved[0], form_z)
    real_k = real_z * kernel
    imag_k = imag_z * kernel
    back_real = along(cos_z, real_k, form_z) - along(sin_z, imag_k, form_z)
    back_imag = along(cos_z, imag_k, form_z) + along(sin_z, real_k, form_z)
    return jnp.stack([back_real, back_imag])


def solve_hartree(net, depth):
    planes, rows, cols = net.shape
    cos_x, sin_x = tables(cols)
    cos_y, sin_y = tables(rows)
    cos_z, sin_z = tables(depth)
    local_rows = rows // lax.axis_size("grid")
    row_index = lax.axis_index("grid") * local_rows + jnp.arange(local_rows, dtype=jnp.int32)
    real_x = jnp.dot(net, cos_x, precision=highest)
    imag_x = -jnp.dot(net, sin_x, precision=highest)
    real_y, imag_y = forward_y(cos_y, sin_y, real_x, imag_x)
    moved = lax.all_to_all(
        jnp.stack([real_y, imag_y]), "grid", split_axis=2, concat_axis=1, tiled=True
    )
    kernel = kernel_at(depth, row_index, rows, jnp.arange(cols, dtype=jnp.int32), cols)
    back = z_kernel(cos_z, sin_z, moved, kernel)
    returned = lax.all_to_all(back, "grid", split_axis=1, concat_axis=2, tiled=True)
    plane_real, plane_imag = inverse_y(cos_y, sin_y, returned[0], returned[1])
    result = jnp.dot(plane_real, cos_x, precision=highest) - jnp.dot(
        plane_imag, sin_x, precision=highest
    )
    return result / (cols * rows * depth)


def local(orbitals, occupation, spin_of_band, ionic_charge):
    bands, planes, rows, cols = orbitals.shape
    total = bands * lax.axis_size("band")
    channels = jnp.arange(2, dtype=jnp.int32)
    weights = (
        jnp.where(
            spin_of_band[None, :] == channels[:, None], occupation[None, :].astype(jnp.float32), 0.0
        )
        / total
    )
    values = orbitals.astype(jnp.float32)
    squares = (values * values).reshape(bands, -1)
    partial_value = jnp.dot(weights, squares, precision=highest).reshape(2, planes, rows, cols)
    share = lax.psum_scatter(partial_value, "band", scatter_dimension=2, tiled=True)
    share_rows = share.shape[2]
    ion_share = lax.dynamic_slice_in_dim(
        ionic_charge, lax.axis_index("band") * share_rows, share_rows, 1
    )
    fields = jnp.concatenate(
        [-jnp.cbrt(6.0 / math.pi * share), (share[0] + share[1] - ion_share)[None]], 0
    )
    whole = lax.all_gather(fields, "band", axis=2, tiled=True)
    potential = solve_hartree(whole[2], NZ)[None] + whole[:2]
    pick = (spin_of_band[:, None] == channels[None, :]).astype(jnp.float32)
    chosen = jnp.dot(pick, potential.reshape(2, -1), precision=highest).reshape(
        bands, planes, rows, cols
    )
    applied = (chosen * values).astype(jnp.bfloat16)
    return (potential, applied)


def solution(mesh):
    return jax.shard_map(
        local,
        mesh=mesh,
        in_specs=(P("band", "grid", None, None), P("band"), P("band"), P("grid", None, None)),
        out_specs=(P(None, "grid", None, None), P("band", "grid", None, None)),
        check_vma=False,
    )
```

profile of v0, /device:TPU:0, one launch (start us, length us, event | category | flops | bytes accessed | tf_op | source)
XLA Modules:
  0.0 105.7 jit_solution(1825945070237419519)
XLA Ops:
  7.2 0.0 reduce-scatter.2.cloned.1.call-start
  7.2 0.7 convert_element_type.76
  7.9 3.5 %fusion.1 = f32[2,8,64,128]{3,0,2,1:T(2,128)S(1)} fusion(bf16[8,8,64,128]{3,2,1,0:T(8,128)(2,1)} %param.4, f32[8]{0:T(128)S(1)} %convert_element_type.76, s32[8]{0:T(128)} %param.6), kind=kOutput, calls=%fused_computation.3 | convolution fusion | flops 13631536 | bytes 1572928 | tf_op jit(solution)/shard_map/dot_general | solution.py:96
  11.3 1.1 %copy.29 = f32[2,8,64,128]{3,1,0,2:T(8,128)} copy(f32[2,8,64,128]{3,0,2,1:T(2,128)S(1)} %fusion.1) | data formatting | bytes 1048576 | tf_op jit(solution)/shard_map/dot_general | solution.py:96
  12.4 0.0 reduce-scatter.2.cloned.1.call-update
  12.5 24.7 %reduce-scatter.2.cloned.1.call-done = f32[2,8,16,128]{3,1,0,2:T(8,128)} async-done(((f32[2,8,64,128]{3,1,0,2:T(8,128)}), f32[2,8,16,128]{3,1,0,2:T(8,128)}) %reduce-scatter.2.cloned.1.call-update) | async-done | bytes 131088 | tf_op jit(solution)/shard_map/reduce_scatter | solution.py:97
  37.2 1.0 cbrt_negate_fusion
  38.2 0.9 fusion.34
  39.1 17.2 %all_gather.3 = f32[3,8,64,128]{3,2,1,0:T(8,128)S(1)} all-gather(f32[3,8,16,128]{3,2,1,0:T(8,128)S(1)} %pad_maximum_fusion.2), channel_id=1, replica_groups=mesh['grid'=8,'band'=4] {'band'}, dimensions={2}, use_global_device_ids=true | all-gather | bytes 983040 | tf_op jit(solution)/shard_map/all_gather | solution.py:105
  56.3 0.6 convolution_negate_fusion
  57.0 0.6 fusion.22
  57.6 0.5 fusion.64
  58.1 0.5 fusion.62
  58.6 0.5 fusion.12
  59.2 0.5 fusion.11
  59.8 1.1 %copy.33 = f32[2,8,64,128]{3,1,0,2:T(8,128)} copy(f32[2,8,64,128]{3,2,1,0:T(8,128)S(1)} %pad_maximum_fusion) | data formatting | bytes 1048576 | tf_op jit(solution)/shard_map/stack | solution.py:72
  60.9 3.6 %all-to-all-start = ((f32[2,8,64,128]{3,1,0,2:T(8,128)}), f32[2,8,64,128]{3,1,0,2:T(8,128)S(1)}, u32[]{:S(2)}, u32[]{:S(2)}) async-start(f32[2,8,64,128]{3,1,0,2:T(8,128)} %copy.33), calls=%async_computation.1 | async-start | bytes 1048576 | tf_op jit(solution)/shard_map/all_to_all | solution.py:71
  64.5 0.1 broadcast_add_fusion
  64.6 9.6 %all-to-all-done = f32[2,8,64,128]{3,1,0,2:T(8,128)S(1)} async-done(((f32[2,8,64,128]{3,1,0,2:T(8,128)}), f32[2,8,64,128]{3,1,0,2:T(8,128)S(1)}, u32[]{:S(2)}, u32[]{:S(2)}) %all-to-all-start) | async-done | bytes 524320 | tf_op jit(solution)/shard_map/all_to_all | solution.py:71
  74.3 0.5 fusion.24
  74.8 0.5 fusion.23
  75.3 0.5 fusion.9
  75.8 0.5 fusion.56
  76.3 0.5 fusion.10
  76.9 0.5 fusion.59
  77.4 0.5 fusion.7
  77.9 0.5 fusion.8
  78.5 0.3 copy.35
  78.8 12.1 %all_to_all.30 = f32[2,64,8,128]{3,2,0,1:T(8,128)S(1)} all-to-all(f32[2,64,8,128]{3,2,0,1:T(8,128)S(1)} %copy.35), channel_id=1, replica_groups=mesh['grid'=8,'band'=4] {'grid'}, dimensions={1} | all-to-all | bytes 1048576 | tf_op jit(solution)/shard_map/all_to_all | solution.py:76
  91.0 0.5 fusion.16
  91.5 0.5 fusion.20
  92.1 0.5 fusion.5
  92.6 0.5 fusion.6
  93.1 0.6 fusion.37
  93.8 0.6 fusion.4
  94.4 0.0 copy-start
  94.4 0.0 copy-start.2
  94.4 0.1 slice_add_fusion
  94.5 0.0 copy-start.1
  94.5 0.4 copy.68
  94.9 0.9 copy-done
  95.8 0.0 copy-done.2
  95.8 1.8 %fusion.3 = bf16[8,8,64,128]{3,0,2,1:T(8,128)(2,1)S(1)} fusion(f32[8,64,128,2]{2,3,1,0:T(2,128)S(1)} %bitcast.140, bf16[8,8,64,128]{3,2,1,0:T(8,128)(2,1)S(1)} %copy-done, s32[8]{0:T(128)S(1)} %copy-done.2), kind=kOutput, calls=%fused_computation.4 | convolution fusion | flops 14155792 | bytes 2621472 | tf_op jit(solution)/shard_map/dot_general | solution.py:108
  97.6 0.0 copy-done.1
  97.6 1.2 %copy.39 = bf16[8,8,64,128]{3,2,1,0:T(8,128)(2,1)} copy(bf16[8,8,64,128]{3,0,2,1:T(8,128)(2,1)S(1)} %fusion.3) | data formatting | bytes 2097152
  (9 shorter events, 0.2 us)
Async XLA Ops:
  7.2 30.0 %reduce-scatter.2.cloned.1.call-start = ((), (), s32[]{:S(2)}) async-start(), calls=%async_computation.3 | async-start | bytes 655360 | tf_op jit(solution)/shard_map/reduce_scatter | solution.py:97
  60.9 13.3 %all-to-all-start = ((f32[2,8,64,128]{3,1,0,2:T(8,128)}), f32[2,8,64,128]{3,1,0,2:T(8,128)S(1)}, u32[]{:S(2)}, u32[]{:S(2)}) async-start(f32[2,8,64,128]{3,1,0,2:T(8,128)} %copy.33), calls=%async_computation.1 | async-start | bytes 1048576 | tf_op jit(solution)/shard_map/all_to_all | solution.py:71
  94.4 1.4 %copy-start = (bf16[8,8,64,128]{3,2,1,0:T(8,128)(2,1)S(1)}, bf16[8,8,64,128]{3,2,1,0:T(8,128)(2,1)}, u32[]{:S(2)}) copy-start(bf16[8,8,64,128]{3,2,1,0:T(8,128)(2,1)} %param.4) | copy-start | bytes 3145732
  94.4 1.4 %copy-start.2 = (s32[8]{0:T(128)S(1)}, s32[8]{0:T(128)}, u32[]{:S(2)}) copy-start(s32[8]{0:T(128)} %param.6) | copy-start | bytes 100
  94.5 3.2 %copy-start.1 = (f32[2,8,64,128]{3,2,1,0:T(8,128)}, f32[2,8,64,128]{3,2,1,0:T(8,128)S(1)}, u32[]{:S(2)}) copy-start(f32[2,8,64,128]{3,2,1,0:T(8,128)S(1)} %slice_add_fusion) | copy-start | bytes 1572868
Sparse Core Ops, SparseCore 0:
  12.6 24.5 reduce-scatter.1
where the time goes:
time: 106 us
  waiting for transfers between devices  34.3 us (32%)
  blocking collectives  29.4 us (28%)
  matrix products  16 us (15%)
  between operations  14.3 us (13%)
  local copies, waits for them, and re-layouts  5.2 us (5%)
  starting transfers between devices  3.67 us (3%)
  other arithmetic  2.81 us (3%)
    reduce_scatter x1, waiting for transfers between devices, local(): lax.psum_scatter(partial_value, 'band', scatter_dimension=2, tiled=True)  24.7 us
    all_gather x1, blocking collectives, local(): whole = lax.all_gather(fields, 'band', axis=2, tiled=True)  17.2 us
    all_to_all x1, blocking collectives, solve_hartree(): lax.all_to_all(back, 'grid', split_axis=1, concat_axis=2, tiled=True)  12.1 us
    all_to_all x1, waiting for transfers between devices, solve_hartree(): lax.all_to_all(jnp.stack([real_y, imag_y]), 'grid', split_axis=2, concat_...  9.6 us
    dot_general x16, matrix products, along(): return jnp.einsum(form, table, field, precision=highest)  8.32 us
    all_to_all x1, starting transfers between devices, solve_hartree(): lax.all_to_all(jnp.stack([real_y, imag_y]), 'grid', split_axis=2, concat_...  3.63 us
    dot_general x1, matrix products, local(): jnp.dot(weights, squares, precision=highest).reshape(2, planes, rows, cols)  3.45 us
    unnamed x8, local copies, waits for them, and re-layouts  2.57 us
  transfers between devices with their start and end apart: 2, of which 2 were waited for; matrix products, arithmetic and copies ran while one was open for 0% of the time, Pallas kernels for 0%

commit v1 on v0

--- a/solution.py
+++ b/solution.py
@@ -68,8 +68,14 @@
     real_x = jnp.dot(net, cos_x, precision=highest)
     imag_x = -jnp.dot(net, sin_x, precision=highest)
     real_y, imag_y = forward_y(cos_y, sin_y, real_x, imag_x)
-    moved = lax.all_to_all(
-        jnp.stack([real_y, imag_y]), "grid", split_axis=2, concat_axis=1, tiled=True
+    moved = jnp.concatenate(
+        lax.all_to_all(
+            jnp.stack(jnp.split(jnp.stack([real_y, imag_y]), lax.axis_size("grid"), axis=2)),
+            "grid",
+            0,
+            0,
+        ),
+        axis=1,
     )
     kernel = kernel_at(depth, row_index, rows, jnp.arange(cols, dtype=jnp.int32), cols)
     back = z_kernel(cos_z, sin_z, moved, kernel)

time: 106 us -> 110 us (1.038)
  other arithmetic: 2.81 us -> 7.87 us
  local copies, waits for them, and re-layouts: 5.2 us -> 4.1 us
    unnamed x0 -> x7, other arithmetic: none -> 4.47 us
    another operation x1 -> x0, local copies, waits for them, and re-layouts: 1.1 us -> none  [solve_hartree(): jnp.stack([real_y, imag_y])]
where the time goes in v1:
time: 110 us
  waiting for transfers between devices  34.3 us (31%)
  blocking collectives  29.4 us (27%)
  matrix products  16.1 us (15%)
  between operations  14.3 us (13%)
  other arithmetic  7.87 us (7%)
  local copies, waits for them, and re-layouts  4.1 us (4%)
  starting transfers between devices  3.67 us (3%)
    reduce_scatter x1, waiting for transfers between devices, local(): lax.psum_scatter(partial_value, 'band', scatter_dimension=2, tiled=True)  24.7 us
    all_gather x1, blocking collectives, local(): whole = lax.all_gather(fields, 'band', axis=2, tiled=True)  17.2 us
    all_to_all x1, blocking collectives, solve_hartree(): lax.all_to_all(back, 'grid', split_axis=1, concat_axis=2, tiled=True)  12.1 us
    all_to_all x1, waiting for transfers between devices, solve_hartree(): lax.all_to_all(jnp.stack(jnp.split(jnp.stack([real_y, imag_y]), lax.axis_...  9.6 us
    dot_general x16, matrix products, along(): return jnp.einsum(form, table, field, precision=highest)  8.37 us
    unnamed x7, other arithmetic  4.47 us
    all_to_all x1, starting transfers between devices, solve_hartree(): lax.all_to_all(jnp.stack(jnp.split(jnp.stack([real_y, imag_y]), lax.axis_...  3.63 us
    dot_general x1, matrix products, local(): jnp.dot(weights, squares, precision=highest).reshape(2, planes, rows, cols)  3.45 us
  transfers between devices with their start and end apart: 2, of which 2 were waited for; matrix products, arithmetic and copies ran while one was open for 0% of the time, Pallas kernels for 0%

profile of v1, /device:TPU:0, one launch (start us, length us, event | category | flops | bytes accessed | tf_op | source)
XLA Modules:
  0.0 109.7 jit_solution(12752279769898726653)
XLA Ops:
  7.2 0.0 reduce-scatter.2.cloned.1.call-start
  7.2 0.7 convert_element_type.76
  7.9 3.5 %fusion.1 = f32[2,8,64,128]{3,0,2,1:T(2,128)S(1)} fusion(bf16[8,8,64,128]{3,2,1,0:T(8,128)(2,1)} %param.4, f32[8]{0:T(128)S(1)} %convert_element_type.76, s32[8]{0:T(128)} %param.6), kind=kOutput, calls=%fused_computation.3 | convolution fusion | flops 13631536 | bytes 1572928 | tf_op jit(solution)/shard_map/dot_general | solution.py:102
  11.3 1.1 %copy.35 = f32[2,8,64,128]{3,1,0,2:T(8,128)} copy(f32[2,8,64,128]{3,0,2,1:T(2,128)S(1)} %fusion.1) | data formatting | bytes 1048576 | tf_op jit(solution)/shard_map/dot_general | solution.py:102
  12.4 0.0 reduce-scatter.2.cloned.1.call-update
  12.5 24.7 %reduce-scatter.2.cloned.1.call-done = f32[2,8,16,128]{3,1,0,2:T(8,128)} async-done(((f32[2,8,64,128]{3,1,0,2:T(8,128)}), f32[2,8,16,128]{3,1,0,2:T(8,128)}) %reduce-scatter.2.cloned.1.call-update) | async-done | bytes 131088 | tf_op jit(solution)/shard_map/reduce_scatter | solution.py:103
  37.2 1.0 cbrt_negate_fusion
  38.2 0.9 fusion.61
  39.1 17.2 %all_gather.3 = f32[3,8,64,128]{3,2,1,0:T(8,128)S(1)} all-gather(f32[3,8,16,128]{3,2,1,0:T(8,128)S(1)} %pad_maximum_fusion.1), channel_id=1, replica_groups=mesh['grid'=8,'band'=4] {'band'}, dimensions={2}, use_global_device_ids=true | all-gather | bytes 983040 | tf_op jit(solution)/shard_map/all_gather | solution.py:111
  56.3 0.6 convolution_negate_fusion
  57.0 0.6 fusion.22
  57.6 0.5 fusion.91
  58.1 0.5 fusion.89
  58.6 0.5 fusion.12
  59.2 0.5 fusion.11
  59.7 0.6 fusion.41
  60.3 0.6 fusion.44
  61.0 0.6 fusion.47
  61.6 0.6 fusion.50
  62.3 0.6 fusion.53
  62.9 0.6 fusion.56
  63.5 0.6 fusion.38
  64.2 0.6 fusion.58
  64.8 3.6 %all-to-all-start = ((f32[8,2,8,8,128]{4,3,2,1,0:T(8,128)}), f32[8,2,8,8,128]{4,3,2,1,0:T(8,128)S(1)}, u32[]{:S(2)}, u32[]{:S(2)}) async-start(f32[8,2,8,8,128]{4,3,2,1,0:T(8,128)} %fusion.58), calls=%async_computation.1 | async-start | bytes 1048576 | tf_op jit(solution)/shard_map/all_to_all | solution.py:72
  68.5 0.1 broadcast_add_fusion
  68.6 9.6 %all-to-all-done = f32[8,2,8,8,128]{4,3,2,1,0:T(8,128)S(1)} async-done(((f32[8,2,8,8,128]{4,3,2,1,0:T(8,128)}), f32[8,2,8,8,128]{4,3,2,1,0:T(8,128)S(1)}, u32[]{:S(2)}, u32[]{:S(2)}) %all-to-all-start) | async-done | bytes 524320 | tf_op jit(solution)/shard_map/all_to_all | solution.py:72
  78.2 0.5 fusion.27
  78.7 0.5 fusion.31
  79.3 0.5 fusion.9
  79.8 0.5 fusion.10
  80.4 0.5 fusion.86
  80.9 0.5 fusion.83
  81.4 0.5 fusion.8
  81.9 0.5 fusion.7
  82.5 0.3 copy.43
  82.8 12.1 %all_to_all.20 = f32[2,64,8,128]{3,2,0,1:T(8,128)S(1)} all-to-all(f32[2,64,8,128]{3,2,0,1:T(8,128)S(1)} %copy.43), channel_id=1, replica_groups=mesh['grid'=8,'band'=4] {'grid'}, dimensions={1} | all-to-all | bytes 1048576 | tf_op jit(solution)/shard_map/all_to_all | solution.py:82
  95.0 0.5 fusion.16
  95.5 0.5 fusion.20
  96.1 0.5 fusion.5
  96.6 0.5 fusion.6
  97.1 0.6 fusion.64
  97.8 0.6 fusion.4
  98.4 0.0 copy-start
  98.4 0.1 slice_add_fusion
  98.5 0.4 copy.83
  98.9 0.9 copy-done
  99.8 1.8 %fusion.3 = bf16[8,8,64,128]{3,0,2,1:T(8,128)(2,1)S(1)} fusion(f32[8,64,128,2]{2,3,1,0:T(2,128)S(1)} %bitcast.159, bf16[8,8,64,128]{3,2,1,0:T(8,128)(2,1)S(1)} %copy-done, s32[8]{0:T(128)S(1)} %copy-done.2), kind=kOutput, calls=%fused_computation.4 | convolution fusion | flops 14155792 | bytes 2621472 | tf_op jit(solution)/shard_map/dot_general | solution.py:114
  101.6 1.2 %copy.47 = bf16[8,8,64,128]{3,2,1,0:T(8,128)(2,1)} copy(bf16[8,8,64,128]{3,0,2,1:T(8,128)(2,1)S(1)} %fusion.3) | data formatting | bytes 2097152
  (12 shorter events, 0.2 us)
Async XLA Ops:
  7.2 30.0 %reduce-scatter.2.cloned.1.call-start = ((), (), s32[]{:S(2)}) async-start(), calls=%async_computation.3 | async-start | bytes 655360 | tf_op jit(solution)/shard_map/reduce_scatter | solution.py:103
  64.8 13.3 %all-to-all-start = ((f32[8,2,8,8,128]{4,3,2,1,0:T(8,128)}), f32[8,2,8,8,128]{4,3,2,1,0:T(8,128)S(1)}, u32[]{:S(2)}, u32[]{:S(2)}) async-start(f32[8,2,8,8,128]{4,3,2,1,0:T(8,128)} %fusion.58), calls=%async_computation.1 | async-start | bytes 1048576 | tf_op jit(solution)/shard_map/all_to_all | solution.py:72
  98.4 1.4 %copy-start = (bf16[8,8,64,128]{3,2,1,0:T(8,128)(2,1)S(1)}, bf16[8,8,64,128]{3,2,1,0:T(8,128)(2,1)}, u32[]{:S(2)}) copy-start(bf16[8,8,64,128]{3,2,1,0:T(8,128)(2,1)} %param.4) | copy-start | bytes 3145732
  98.4 1.4 %copy-start.2 = (s32[8]{0:T(128)S(1)}, s32[8]{0:T(128)}, u32[]{:S(2)}) copy-start(s32[8]{0:T(128)} %param.6) | copy-start | bytes 100
  98.5 3.2 %copy-start.1 = (f32[2,8,64,128]{3,2,1,0:T(8,128)}, f32[2,8,64,128]{3,2,1,0:T(8,128)S(1)}, u32[]{:S(2)}) copy-start(f32[2,8,64,128]{3,2,1,0:T(8,128)S(1)} %slice_add_fusion) | copy-start | bytes 1572868
Sparse Core Ops, SparseCore 0:
  12.6 24.5 reduce-scatter.1
